TPU v7x, 512 devices: a whole 4x8x8 slice. The times are simulated.
512 devices in a mesh: dp: 64 (over y, x, core), mp: 8 (over z).
Axes of the slice: x: 4, y: 8, z: 8, core: 2. Of those that a mesh axis runs over, the one named last changes fastest.
Arguments:
- hidden: bfloat16 [960, 128, 2048], P('dp', None, 'mp'), may hold values from -6 to 6
- attn_out: bfloat16 [960, 128, 2048], P('dp', None, 'mp'), may hold values from -6 to 6
- out_proj: bfloat16 [2048, 2048], P(None, 'mp'), may hold values from -0.125 to 0.125
- norm_gain: float32 [2048], P('mp'), may hold values from 0.1 to 1.9
- reward_proj: float32 [2048, 8], P('mp'), may hold values from -0.125 to 0.125
- block_seq: int32 [960], replicated, may hold values from -1 to 383, as said below
- block_dest: int32 [960], replicated, may hold values from -1 to 639, as said below
- lengths: int32 [384], replicated, may hold values from 1 to 512, as said below
Outputs:
- token_rewards: float32 [640, 8, 128], P('dp')
- advantages: float32 [384], P('dp')
Inputs may be any that keep to these rules, and one draw needn't show every extreme that they name: `block_seq`: used slots of each index of dp come first in its 15 slots, the rest hold -1; each index of dp holds 1 to 15 used slots and some index holds exactly 15. Read over used slots in slot order, response numbers never fall, every response appears, and each has 1 to 4 blocks. `block_dest`: exactly the used slots (those of block_seq that are not -1) hold a destination; every owned slot of every owner is named exactly once, so each owner receives exactly 10 blocks; at most 1 block go from one index of dp to one owner, and that many in some pair. `lengths`: A response of n blocks has more than 128 * (n - 1) and at most 128 * n tokens.
All inputs are finite; a program needn't handle non-finite values.
Results may differ from a plain program's by a relative error of at most 0.0029.
Values may be sent and summed in bfloat16 or wider, within the bound.
No kernel may reach another device: no remote copies, remote signals or barrier semaphores. Data moves between devices by JAX's collectives and lax.ppermute only.
A program may use at most 64 MiB of HBM per device.

v0:
```python
import jax
import jax.numpy as jnp
from jax import lax
from jax.sharding import PartitionSpec as P

OWN_CAP = 10
norm_epsilon = 1e-05
stat_epsilon = 1e-06


def sent_to_all(value, axis):
    copies = jnp.broadcast_to(value, (lax.axis_size(axis), *value.shape))
    return lax.all_to_all(copies, axis, split_axis=0, concat_axis=0, tiled=True)


def of_everyone(value, axis):
    everything = sent_to_all(value, axis)
    return jnp.sum(everything, axis=0)


def packed_total(arrays, axis):
    ends = [0]
    for a in arrays:
        ends.append(ends[-1] + a.size)
    so_far = of_everyone(jnp.concatenate([a.ravel() for a in arrays]), axis)
    return tuple((so_far[b:e].reshape(a.shape) for a, b, e in zip(arrays, ends, ends[1:])))


def split_up(value, dim, peers):
    before, after = (value.shape[:dim], value.shape[dim + 1 :])
    return jnp.moveaxis(value.reshape(*before, peers, -1, *after), dim, 0)


def sent_and_summed(value, axis, dim):
    parts = split_up(value, dim, lax.axis_size(axis))
    arrived = lax.all_to_all(parts, axis, split_axis=0, concat_axis=0, tiled=True)
    return arrived.sum(axis=0)


def local(hidden, attn_out, out_proj, norm_gain, reward_proj, block_seq, block_dest, lengths):
    device_count = lax.axis_size("dp")
    device_rank = lax.axis_index("dp")
    slots_in = hidden.shape[0]
    block_len = hidden.shape[1]
    model_width = out_proj.shape[0]
    seq_count = lengths.shape[0]
    seq_local = seq_count // device_count
    slot_depth = (slots_in + device_count - 1) // device_count
    all_slots = jnp.arange(block_dest.shape[0], dtype=jnp.int32)
    local_dest = lax.dynamic_slice_in_dim(block_dest, device_rank * slots_in, slots_in)
    is_used = local_dest >= 0
    owner_rank = jnp.where(is_used, local_dest // OWN_CAP, -1)
    local_slots = jnp.arange(slots_in, dtype=jnp.int32)
    earlier = (
        (owner_rank[None, :] == owner_rank[:, None])
        & (local_slots[None, :] < local_slots[:, None])
        & is_used[None, :]
    )
    send_row = jnp.where(is_used, owner_rank * slot_depth + earlier.sum(axis=1), -1)
    buffer_rows = jnp.arange(device_count * slot_depth, dtype=jnp.int32)
    selector = (send_row[None, :] == buffer_rows[:, None]).astype(jnp.bfloat16)
    targets = device_rank * OWN_CAP + jnp.arange(OWN_CAP, dtype=jnp.int32)
    matches = block_dest[None, :] == targets[:, None]
    source_slot = jnp.sum(jnp.where(matches, all_slots[None, :], 0), axis=1)
    source_rank = source_slot // slots_in
    before = (block_dest[None, :] >= 0) & (block_dest[None, :] // OWN_CAP == device_rank)
    before = (
        before
        & (all_slots[None, :] >= (source_rank * slots_in)[:, None])
        & (all_slots[None, :] < source_slot[:, None])
    )
    recv_row = source_rank * slot_depth + before.sum(axis=1)
    seq_own = jnp.sum(jnp.where(matches, block_seq[None, :], 0), axis=1)
    earlier_same = (block_seq[None, :] == seq_own[:, None]) & (
        all_slots[None, :] < source_slot[:, None]
    )
    seq_rank = earlier_same.sum(axis=1)
    seq_ids = jnp.arange(seq_count, dtype=jnp.int32)
    member = seq_ids[:, None] == seq_own[None, :]
    own_length = jnp.sum(jnp.where(member, lengths[:, None], 0), axis=0)
    valid_tokens = jnp.minimum(block_len, own_length - block_len * seq_rank)
    projected = jnp.einsum(
        "btf,fc->btc",
        lax.all_gather(attn_out, "mp", axis=2, tiled=True),
        out_proj,
        preferred_element_type=jnp.float32,
    )
    local_resid = (hidden.astype(jnp.float32) + projected).astype(jnp.bfloat16)
    moved_resid = lax.all_to_all(
        jnp.einsum("rj,jtf->rtf", selector, local_resid, preferred_element_type=jnp.float32).astype(
            jnp.bfloat16
        ),
        "dp",
        split_axis=0,
        concat_axis=0,
        tiled=True,
    )
    residual = jnp.take(moved_resid, recv_row, axis=0)
    values = residual.astype(jnp.float32)
    squares = jnp.sum(values * values, axis=2)
    weighted = norm_gain[:, None] * reward_proj
    partial_value = jnp.einsum("btf,fh->bht", values, weighted, precision=lax.Precision.HIGHEST)
    squares, partial_value = packed_total((squares, partial_value), "mp")
    inverse_rms = lax.rsqrt(squares / model_width + norm_epsilon)
    live_tokens = (jnp.arange(block_len, dtype=jnp.int32)[None, :] < valid_tokens[:, None]).astype(
        jnp.float32
    )
    token_rewards = partial_value * (inverse_rms * live_tokens)[:, None, :]
    block_sums = jnp.sum(token_rewards, axis=2)
    seq_part = jnp.dot(member.astype(jnp.float32), block_sums, precision=lax.Precision.HIGHEST)
    seq_totals = sent_and_summed(seq_part, "dp", 0)
    own_lengths = lax.dynamic_slice_in_dim(lengths, device_rank * seq_local, seq_local).astype(
        jnp.float32
    )
    scores = seq_totals / own_lengths[:, None]
    worst_case = jnp.min(scores, axis=1)
    head_mean = jnp.mean(scores, axis=1)
    spread = jnp.mean((scores - head_mean[:, None]) ** 2, axis=1)
    total_seqs = float(seq_count)
    moment_sums = packed_total(
        (
            jnp.sum(spread),
            jnp.sum(worst_case),
            jnp.sum(worst_case * worst_case),
            jnp.sum(worst_case * spread),
            jnp.sum(spread * spread),
        ),
        "dp",
    )
    penalty_scale = moment_sums[0] / total_seqs + stat_epsilon
    conservative = worst_case - spread / penalty_scale
    first_sum = moment_sums[1] - moment_sums[0] / penalty_scale
    second = (
        moment_sums[2]
        - 2.0 * moment_sums[3] / penalty_scale
        + moment_sums[4] / (penalty_scale * penalty_scale)
    )
    centre = first_sum / total_seqs
    variance = second / total_seqs - centre * centre
    advantages = (conservative - centre) * lax.rsqrt(variance + stat_epsilon)
    return (token_rewards, advantages)


def solution(mesh):
    return jax.shard_map(
        local,
        mesh=mesh,
        in_specs=(
            P("dp", None, "mp"),
            P("dp", None, "mp"),
            P(None, "mp"),
            P("mp"),
            P("mp", None),
            P(),
            P(),
            P(),
        ),
        out_specs=(P("dp", None, None), P("dp")),
        check_vma=False,
    )
```

profile of v0, /device:TPU:1, one launch (start us, length us, event | category | flops | bytes accessed | tf_op | source)
XLA Modules:
  0.0 305.1 jit_solution(17338030331236136521)
XLA Ops:
  7.2 0.7 all-gather.2.cloned.1.call-update
  7.9 0.8 fusion.29
  8.9 101.2 %all-gather.2.cloned.1.call-done = bf16[15,128,2048]{2,1,0:T(8,128)(2,1)} async-done(((bf16[15,128,256]{2,1,0:T(8,128)(2,1)}), bf16[15,128,2048]{2,1,0:T(8,128)(2,1)}) %all-gather.2.cloned.1.call-update) | async-done | bytes 7864336 | tf_op jit(solution)/shard_map/all_gather | solution.py:84
  110.1 5.7 %add_convert_fusion = bf16[15,128,256]{2,1,0:T(8,128)(2,1)S(1)} fusion(bf16[15,128,256]{2,1,0:T(8,128)(2,1)} %param.8, bf16[15,128,2048]{2,1,0:T(8,128)(2,1)} %all-gather.2.cloned.1.call-done, bf16[2048,256]{1,0:T(8,128)(2,1)S(1)} %copy-done), kind=kOutput, calls=%fused_computation.3 | convolution fusion | flops 2014740480 | bytes 10878976 | tf_op jit(solution)/shard_map/btf,fc->btc/dot_general | solution.py:82
  115.8 1.4 convolution_convert_fusion
  117.1 4.4 %copy.29 = bf16[64,128,256]{2,1,0:T(8,128)(2,1)} copy(bf16[64,128,256]{2,0,1:T(8,128)(2,1)S(1)} %convolution_convert_fusion) | data formatting | bytes 8388608 | tf_op jit(solution)/shard_map/convert_element_type | solution.py:90
  121.5 13.3 %all-to-all-start = ((bf16[64,128,256]{2,1,0:T(8,128)(2,1)}), bf16[64,128,256]{2,1,0:T(8,128)(2,1)}, u32[]{:S(2)}, u32[]{:S(2)}) async-start(bf16[64,128,256]{2,1,0:T(8,128)(2,1)} %copy.29), calls=%async_computation | async-start | bytes 8388608 | tf_op jit(solution)/shard_map/all_to_all | solution.py:89
  135.4 94.2 %all-to-all-done = bf16[64,128,256]{2,1,0:T(8,128)(2,1)} async-done(((bf16[64,128,256]{2,1,0:T(8,128)(2,1)}), bf16[64,128,256]{2,1,0:T(8,128)(2,1)}, u32[]{:S(2)}, u32[]{:S(2)}) %all-to-all-start) | async-done | bytes 4194336 | tf_op jit(solution)/shard_map/all_to_all | solution.py:89
  229.5 2.8 gather_fusion
  232.3 0.3 multiply_reduce_fusion
  232.7 0.7 convolution_bitcast_fusion
  233.4 0.9 broadcast_in_dim.89
  234.3 3.9 %all-to-all-start.1 = ((f32[8,1,11520]{2,1,0:T(1,128)}), f32[8,1,11520]{2,1,0:T(1,128)S(1)}, u32[]{:S(2)}, u32[]{:S(2)}) async-start(f32[8,1,11520]{2,1,0:T(1,128)} %broadcast_in_dim.89), calls=%async_computation.1 | async-start | bytes 737280 | tf_op jit(solution)/shard_map/all_to_all | solution.py:13
  238.4 11.5 %all-to-all-done.1 = f32[8,1,11520]{2,1,0:T(1,128)S(1)} async-done(((f32[8,1,11520]{2,1,0:T(1,128)}), f32[8,1,11520]{2,1,0:T(1,128)S(1)}, u32[]{:S(2)}, u32[]{:S(2)}) %all-to-all-start.1) | async-done | bytes 368672 | tf_op jit(solution)/shard_map/all_to_all | solution.py:13
  249.9 0.3 reduce_sum.169
  250.2 0.6 fusion.34
  251.1 0.8 copy.32
  251.9 9.6 %all-to-all-start.2 = ((f32[64,6,8]{2,1,0:T(8,128)}), f32[64,6,8]{2,1,0:T(8,128)S(1)}, u32[]{:S(2)}, u32[]{:S(2)}) async-start(f32[64,6,8]{2,1,0:T(8,128)} %copy.32), calls=%async_computation.2 | async-start | bytes 524288 | tf_op jit(solution)/shard_map/all_to_all | solution.py:36
  261.6 13.0 %all-to-all-done.2 = f32[64,6,8]{2,1,0:T(8,128)S(1)} async-done(((f32[64,6,8]{2,1,0:T(8,128)}), f32[64,6,8]{2,1,0:T(8,128)S(1)}, u32[]{:S(2)}, u32[]{:S(2)}) %all-to-all-start.2) | async-done | bytes 12320 | tf_op jit(solution)/shard_map/all_to_all | solution.py:36
  275.1 0.7 multiply_reduce_fusion.2
  275.8 3.2 %concatenate.7 = f32[5]{0:T(128)S(1)} concatenate(f32[1]{0:T(128)} %bitcast.13, f32[1]{0:T(128)} %bitcast.14, f32[1]{0:T(128)} %bitcast.15, f32[1]{0:T(128)} %bitcast.16, f32[1]{0:T(128)} %bitcast.17), dimensions={0} | concatenate | bytes 40 | tf_op jit(solution)/shard_map/concatenate | solution.py:25
  279.1 14.0 %all_to_all.22 = f32[64,1,5]{2,1,0:T(1,128)S(1)} all-to-all(f32[64,1,5]{2,1,0:T(1,128)S(1)} %broadcast_in_dim.93), channel_id=1, replica_groups=mesh['dp'=64,'mp'=8] {'dp'}, dimensions={0} | all-to-all | bytes 2560 | tf_op jit(solution)/shard_map/all_to_all | solution.py:13
  293.1 0.7 fusion.36
  297.7 0.5 subtract_multiply_fusion
  (36 shorter events, 1.9 us)
Async XLA Ops:
  7.2 102.9 %copy-start = (bf16[2048,256]{1,0:T(8,128)(2,1)S(1)}, bf16[2048,256]{1,0:T(8,128)(2,1)}, u32[]{:S(2)}) copy-start(bf16[2048,256]{1,0:T(8,128)(2,1)} %param.10) | copy-start | bytes 3145732
  7.2 102.9 %all-gather.2.cloned.1.call-start = ((), (), s32[]{:S(2)}) async-start(), calls=%async_computation.4 | async-start | bytes 8847360 | tf_op jit(solution)/shard_map/all_gather | solution.py:84
  121.5 13.3 %copy-start.1 = (s32[960]{0:T(1024)S(1)}, s32[960]{0:T(1024)}, u32[]{:S(2)}) copy-start(s32[960]{0:T(1024)} %param.14) | copy-start | bytes 11524
  121.5 13.3 %copy-start.2 = (s32[960]{0:T(1024)S(1)}, s32[960]{0:T(1024)}, u32[]{:S(2)}) copy-start(s32[960]{0:T(1024)} %param.13) | copy-start | bytes 11524
  121.5 111.1 %copy-start.4 = (f32[256,8]{0,1:T(8,128)S(1)}, f32[256,8]{0,1:T(8,128)}, u32[]{:S(2)}) copy-start(f32[256,8]{0,1:T(8,128)} %param.12) | copy-start | bytes 24580
  121.5 111.1 %copy-start.5 = (f32[256]{0:T(256)S(1)}, f32[256]{0:T(256)}, u32[]{:S(2)}) copy-start(f32[256]{0:T(256)} %param.11) | copy-start | bytes 3076
  121.5 108.0 %all-to-all-start = ((bf16[64,128,256]{2,1,0:T(8,128)(2,1)}), bf16[64,128,256]{2,1,0:T(8,128)(2,1)}, u32[]{:S(2)}, u32[]{:S(2)}) async-start(bf16[64,128,256]{2,1,0:T(8,128)(2,1)} %copy.29), calls=%async_computation | async-start | bytes 8388608 | tf_op jit(solution)/shard_map/all_to_all | solution.py:89
  134.8 103.4 %copy-start.3 = (s32[384]{0:T(512)S(1)}, s32[384]{0:T(512)}, u32[]{:S(2)}) copy-start(s32[384]{0:T(512)} %param.15) | copy-start | bytes 4612
  234.3 15.6 %all-to-all-start.1 = ((f32[8,1,11520]{2,1,0:T(1,128)}), f32[8,1,11520]{2,1,0:T(1,128)S(1)}, u32[]{:S(2)}, u32[]{:S(2)}) async-start(f32[8,1,11520]{2,1,0:T(1,128)} %broadcast_in_dim.89), calls=%async_computation.1 | async-start | bytes 737280 | tf_op jit(solution)/shard_map/all_to_all | solution.py:13
  251.9 22.7 %all-to-all-start.2 = ((f32[64,6,8]{2,1,0:T(8,128)}), f32[64,6,8]{2,1,0:T(8,128)S(1)}, u32[]{:S(2)}, u32[]{:S(2)}) async-start(f32[64,6,8]{2,1,0:T(8,128)} %copy.32), calls=%async_computation.2 | async-start | bytes 524288 | tf_op jit(solution)/shard_map/all_to_all | solution.py:36
Sparse Core Ops, SparseCore 0:
  10.0 100.0 all-gather.1
where the time goes:
time: 306 us; the launch traced here: 305 us
  waiting for transfers between devices  221 us (72%)
  starting transfers between devices  26.8 us (9%)
  between operations  18.1 us (6%)
  blocking collectives  14 us (5%)
  local copies, waits for them, and re-layouts  12.9 us (4%)
  matrix products  7.93 us (3%)
  other arithmetic  4.83 us (2%)
    all_gather x1, waiting for transfers between devices, local(): lax.all_gather(attn_out, 'mp', axis=2, tiled=True)  101 us
    all_to_all x1, waiting for transfers between devices, local(): lax.all_to_all(jnp.einsum('rj,jtf->rtf', selector, local_resid, preferred...  94.2 us
    all_to_all x1, blocking collectives, sent_to_all(): return lax.all_to_all(copies, axis, split_axis=0, concat_axis=0, tiled=True)  14 us
    all_to_all x1, starting transfers between devices, local(): lax.all_to_all(jnp.einsum('rj,jtf->rtf', selector, local_resid, preferred...  13.3 us
    all_to_all x1, waiting for transfers between devices, sent_and_summed(): lax.all_to_all(parts, axis, split_axis=0, concat_axis=0, tiled=True)  13 us
    all_to_all x1, waiting for transfers between devices, sent_to_all(): return lax.all_to_all(copies, axis, split_axis=0, concat_axis=0, tiled=True)  11.5 us
    all_to_all x1, starting transfers between devices, sent_and_summed(): lax.all_to_all(parts, axis, split_axis=0, concat_axis=0, tiled=True)  9.64 us
  transfers between devices with their start and end apart: 4, of which 4 were waited for; matrix products, arithmetic and copies ran while one was open for 1% of the time, Pallas kernels for 0%

commit v1 on v0

--- a/solution.py
+++ b/solution.py
@@ -1,3 +1,4 @@
+import functools
 import jax
 import jax.numpy as jnp
 from jax import lax
@@ -6,6 +7,39 @@
 OWN_CAP = 10
 norm_epsilon = 1e-05
 stat_epsilon = 1e-06
+
+
+def pair_the_yards(s0, out_dim):
+    s0 = jnp.moveaxis(s0, 0, out_dim)
+    p_next = s0.shape
+    return s0.reshape(
+        *p_next[:out_dim], p_next[out_dim] * p_next[out_dim + 1], *p_next[out_dim + 2 :]
+    )
+
+
+def raise_axis_part(xx, row_axis):
+    f_now, field_out = (lax.axis_size(row_axis), lax.axis_index(row_axis))
+    far_arr, finding = (xx[None], 1)
+    while finding < f_now:
+        runs = []
+        ii = 0
+        while ii < f_now:
+            runs.append((ii, ii ^ finding))
+            ii += 1
+        arr_out = lax.ppermute(far_arr, axis_name=row_axis, perm=runs)
+        wide_out = field_out & finding == 0
+        far_arr = jnp.concatenate(
+            [jnp.where(wide_out, far_arr, arr_out), jnp.where(wide_out, arr_out, far_arr)]
+        )
+        finding *= 2
+    return far_arr
+
+
+def mix_the_copies(vals, local_values, axis_k):
+    return pair_the_yards(raise_axis_part(vals, local_values), axis_k)
+
+
+end_the_seats_all = functools.partial(mix_the_copies, local_values="mp", axis_k=2)
 
 
 def sent_to_all(value, axis):
@@ -80,10 +114,7 @@
     own_length = jnp.sum(jnp.where(member, lengths[:, None], 0), axis=0)
     valid_tokens = jnp.minimum(block_len, own_length - block_len * seq_rank)
     projected = jnp.einsum(
-        "btf,fc->btc",
-        lax.all_gather(attn_out, "mp", axis=2, tiled=True),
-        out_proj,
-        preferred_element_type=jnp.float32,
+        "btf,fc->btc", end_the_seats_all(attn_out), out_proj, preferred_element_type=jnp.float32
     )
     local_resid = (hidden.astype(jnp.float32) + projected).astype(jnp.bfloat16)
     moved_resid = lax.all_to_all(

time: 306 us -> 504 us (1.65)
  waiting for transfers between devices: 221 us -> 390 us
  starting transfers between devices: 26.8 us -> 50 us
  other arithmetic: 4.83 us -> 21.5 us
  between operations: 18.1 us -> 4.79 us
    ppermute x0 -> x3, waiting for transfers between devices: none -> 271 us  [raise_axis_part(): arr_out = lax.ppermute(far_arr, axis_name=row_axis, perm=runs)]
    all_gather x1 -> x0, waiting for transfers between devices: 101 us -> none  [local(): lax.all_gather(attn_out, 'mp', axis=2, tiled=True)]
    ppermute x0 -> x3, starting transfers between devices: none -> 22.8 us  [raise_axis_part(): arr_out = lax.ppermute(far_arr, axis_name=row_axis, perm=runs)]
    concatenate x0 -> x3, other arithmetic: none -> 9.78 us  [raise_axis_part(): jnp.concatenate([jnp.where(wide_out, far_arr, arr_out), jnp.where(wide_ou...]
    select_n x0 -> x3, other arithmetic: none -> 7.59 us  [raise_axis_part(): jnp.where(wide_out, far_arr, arr_out)]
  transfers between devices with their start and end apart: 4 -> 6, of which waited for: 4 -> 6; matrix products, arithmetic and copies ran while one was open for 1% -> 0% of each run, Pallas kernels for 0% -> 0%
where the time goes in v1:
time: 504 us; the launch traced here: 503 us
  waiting for transfers between devices  390 us (77%)
  starting transfers between devices  50 us (10%)
  other arithmetic  21.5 us (4%)
  local copies, waits for them, and re-layouts  15.6 us (3%)
  blocking collectives  14 us (3%)
  matrix products  7.76 us (2%)
    ppermute x3, waiting for transfers between devices, raise_axis_part(): arr_out = lax.ppermute(far_arr, axis_name=row_axis, perm=runs)  271 us
    all_to_all x1, waiting for transfers between devices, local(): lax.all_to_all(jnp.einsum('rj,jtf->rtf', selector, local_resid, preferred...  94.2 us
    ppermute x3, starting transfers between devices, raise_axis_part(): arr_out = lax.ppermute(far_arr, axis_name=row_axis, perm=runs)  22.8 us
    all_to_all x1, blocking collectives, sent_to_all(): return lax.all_to_all(copies, axis, split_axis=0, concat_axis=0, tiled=True)  14 us
    all_to_all x1, waiting for transfers between devices, sent_and_summed(): lax.all_to_all(parts, axis, split_axis=0, concat_axis=0, tiled=True)  13 us
    all_to_all x1, starting transfers between devices, local(): lax.all_to_all(jnp.einsum('rj,jtf->rtf', selector, local_resid, preferred...  12.5 us
    all_to_all x1, waiting for transfers between devices, sent_to_all(): return lax.all_to_all(copies, axis, split_axis=0, concat_axis=0, tiled=True)  11.5 us
  transfers between devices with their start and end apart: 6, of which 6 were waited for; matrix products, arithmetic and copies ran while one was open for 0% of the time, Pallas kernels for 0%

profile of v1, /device:TPU:1, one launch (start us, length us, event | category | flops | bytes accessed | tf_op | source)
XLA Modules:
  0.0 503.3 jit_solution(7355960474131697853)
XLA Ops:
  0.6 1.7 copy.35
  2.3 4.8 collective-permute-start
  7.2 17.4 %collective-permute-done = bf16[1,15,128,256]{2,3,0,1:T(8,128)(2,1)S(1)} collective-permute-done((bf16[1,15,128,256]{2,3,0,1:T(8,128)(2,1)S(1)}, bf16[1,15,128,256]{2,3,0,1:T(8,128)(2,1)S(1)}, u32[]{:S(2)}, u32[]{:S(2)}) %collective-permute-start) | collective-permute-done | bytes 983072 | tf_op jit(solution)/shard_map/ppermute | solution.py:29
  24.7 0.9 copy-done.2
  26.0 9.8 %collective-permute-start.1 = (bf16[2,15,128,256]{2,3,0,1:T(8,128)(2,1)S(1)}, bf16[2,15,128,256]{2,3,0,1:T(8,128)(2,1)}, u32[]{:S(2)}, u32[]{:S(2)}) collective-permute-start(bf16[2,15,128,256]{2,3,0,1:T(8,128)(2,1)S(1)} %pad_maximum_fusion.2), channel_id=1, source_target_pairs={{0,2},{1,3},{2,0},{3,1},{4,6},{5,7},{6,4},{7,5},{8,10},{9,11},{10,... | collective-permute-start | bytes 5898248 | tf_op jit(solution)/shard_map/ppermute | solution.py:29
  35.8 84.6 %collective-permute-done.1 = bf16[2,15,128,256]{2,3,0,1:T(8,128)(2,1)} collective-permute-done((bf16[2,15,128,256]{2,3,0,1:T(8,128)(2,1)S(1)}, bf16[2,15,128,256]{2,3,0,1:T(8,128)(2,1)}, u32[]{:S(2)}, u32[]{:S(2)}) %collective-permute-start.1) | collective-permute-done | bytes 1966112 | tf_op jit(solution)/shard_map/ppermute | solution.py:29
  120.4 2.3 broadcast_select_fusion.3
  122.8 2.5 pad_maximum_fusion.1
  125.3 8.1 %collective-permute-start.2 = (bf16[4,15,128,256]{2,3,0,1:T(8,128)(2,1)}, bf16[4,15,128,256]{2,3,0,1:T(8,128)(2,1)}, u32[]{:S(2)}, u32[]{:S(2)}) collective-permute-start(bf16[4,15,128,256]{2,3,0,1:T(8,128)(2,1)} %pad_maximum_fusion.1), channel_id=1, source_target_pairs={{0,4},{1,5},{2,6},{3,7},{4,0},{5,1},{6,2},{7,3},{8,12},{9,13},{10,... | collective-permute-start | bytes 11796488 | tf_op jit(solution)/shard_map/ppermute | solution.py:29
  133.7 168.9 %collective-permute-done.2 = bf16[4,15,128,256]{2,3,0,1:T(8,128)(2,1)} collective-permute-done((bf16[4,15,128,256]{2,3,0,1:T(8,128)(2,1)}, bf16[4,15,128,256]{2,3,0,1:T(8,128)(2,1)}, u32[]{:S(2)}, u32[]{:S(2)}) %collective-permute-start.2) | collective-permute-done | bytes 3932192 | tf_op jit(solution)/shard_map/ppermute | solution.py:29
  302.7 5.1 %broadcast_select_fusion.1 = (bf16[4,15,128,256]{2,3,0,1:T(8,128)(2,1)}, bf16[4,15,128,256]{2,3,0,1:T(8,128)(2,1)}) fusion(bf16[4,15,128,256]{2,3,0,1:T(8,128)(2,1)} %collective-permute-done.2, pred[]{:T(512)S(6)} %eq.103, bf16[2,15,128,256]{2,3,0,1:T(8,128)(2,1)} %copy-done.1, bf16[2,15,128,256]{2,3,0,1:T(8,128)(2,1)S(1)} %get-tuple-element.21), kind=kLoop, calls=%fused_computation.4 | loop fusion | flops 5898240 | bytes 15728641 | tf_op jit(solution)/shard_map/jit(_where)/select_n | solution.py:32
  307.8 7.1 %pad_maximum_fusion = bf16[8,15,128,256]{2,3,0,1:T(8,128)(2,1)} fusion(bf16[4,15,128,256]{2,3,0,1:T(8,128)(2,1)} %get-tuple-element.20, bf16[4,15,128,256]{2,3,0,1:T(8,128)(2,1)} %get-tuple-element.19), kind=kLoop, calls=%fused_computation.1 | loop fusion | flops 3932160 | bytes 15728640 | tf_op jit(solution)/shard_map/concatenate | solution.py:31
  314.9 5.5 %add_convert_fusion = bf16[15,128,256]{2,1,0:T(8,128)(2,1)S(1)} fusion(bf16[15,128,256]{2,1,0:T(8,128)(2,1)S(1)} %copy-done.4, bf16[15,128,2048]{1,2,0:T(8,128)(2,1)} %bitcast.59, bf16[2048,256]{1,0:T(8,128)(2,1)S(1)} %copy-done), kind=kOutput, calls=%fused_computation.8 | convolution fusion | flops 2014740480 | bytes 10878976 | tf_op jit(solution)/shard_map/btf,fc->btc/dot_general | solution.py:116
  320.4 1.4 convolution_convert_fusion
  321.8 4.4 copy.38
  326.2 12.5 %all-to-all-start = ((bf16[64,128,256]{2,1,0:T(8,128)(2,1)}), bf16[64,128,256]{2,1,0:T(8,128)(2,1)}, u32[]{:S(2)}, u32[]{:S(2)}) async-start(bf16[64,128,256]{2,1,0:T(8,128)(2,1)} %copy.38), calls=%async_computation | async-start | bytes 8388608 | tf_op jit(solution)/shard_map/all_to_all | solution.py:120
  339.2 94.2 %all-to-all-done = bf16[64,128,256]{2,1,0:T(8,128)(2,1)} async-done(((bf16[64,128,256]{2,1,0:T(8,128)(2,1)}), bf16[64,128,256]{2,1,0:T(8,128)(2,1)}, u32[]{:S(2)}, u32[]{:S(2)}) %all-to-all-start) | async-done | bytes 4194336 | tf_op jit(solution)/shard_map/all_to_all | solution.py:120
  433.4 2.8 gather_fusion
  438.1 5.2 %all-to-all-start.1 = ((f32[8,1,11520]{2,1,0:T(1,128)}), f32[8,1,11520]{2,1,0:T(1,128)S(1)}, u32[]{:S(2)}, u32[]{:S(2)}) async-start(f32[8,1,11520]{2,1,0:T(1,128)} %broadcast_in_dim.93), calls=%async_computation.1 | async-start | bytes 737280 | tf_op jit(solution)/shard_map/all_to_all | solution.py:47
  443.5 11.5 %all-to-all-done.1 = f32[8,1,11520]{2,1,0:T(1,128)S(1)} async-done(((f32[8,1,11520]{2,1,0:T(1,128)}), f32[8,1,11520]{2,1,0:T(1,128)S(1)}, u32[]{:S(2)}, u32[]{:S(2)}) %all-to-all-start.1) | async-done | bytes 368672 | tf_op jit(solution)/shard_map/all_to_all | solution.py:47
  457.0 9.6 %all-to-all-start.2 = ((f32[64,6,8]{2,1,0:T(8,128)}), f32[64,6,8]{2,1,0:T(8,128)S(1)}, u32[]{:S(2)}, u32[]{:S(2)}) async-start(f32[64,6,8]{2,1,0:T(8,128)} %copy.41), calls=%async_computation.2 | async-start | bytes 524288 | tf_op jit(solution)/shard_map/all_to_all | solution.py:70
  466.7 13.0 %all-to-all-done.2 = f32[64,6,8]{2,1,0:T(8,128)S(1)} async-done(((f32[64,6,8]{2,1,0:T(8,128)}), f32[64,6,8]{2,1,0:T(8,128)S(1)}, u32[]{:S(2)}, u32[]{:S(2)}) %all-to-all-start.2) | async-done | bytes 12320 | tf_op jit(solution)/shard_map/all_to_all | solution.py:70
  480.9 3.2 concatenate.19
  484.2 14.0 %all_to_all.22 = f32[64,1,5]{2,1,0:T(1,128)S(1)} all-to-all(f32[64,1,5]{2,1,0:T(1,128)S(1)} %broadcast_in_dim.97), channel_id=1, replica_groups=mesh['dp'=64,'mp'=8] {'dp'}, dimensions={0} | all-to-all | bytes 2560 | tf_op jit(solution)/shard_map/all_to_all | solution.py:47
  (54 shorter events, 8.0 us)
Async XLA Ops:
  0.6 314.3 %copy-start = (bf16[2048,256]{1,0:T(8,128)(2,1)S(1)}, bf16[2048,256]{1,0:T(8,128)(2,1)}, u32[]{:S(2)}) copy-start(bf16[2048,256]{1,0:T(8,128)(2,1)} %param.10) | copy-start | bytes 3145732
  2.3 22.3 %collective-permute-start = (bf16[1,15,128,256]{2,3,0,1:T(8,128)(2,1)S(1)}, bf16[1,15,128,256]{2,3,0,1:T(8,128)(2,1)S(1)}, u32[]{:S(2)}, u32[]{:S(2)}) collective-permute-start(bf16[1,15,128,256]{2,3,0,1:T(8,128)(2,1)S(1)} %bitcast.60), channel_id=1, source_target_pairs={{0,1},{1,0},{2,3},{3,2},{4,5},{5,4},{6,7},{7,6},{8,9},{9,8},{10,11... | collective-permute-start | bytes 2949128 | tf_op jit(solution)/shard_map/ppermute | solution.py:29
  24.7 0.9 copy-start.2
  24.7 1.3 copy-start.3
  26.0 94.4 %collective-permute-start.1 = (bf16[2,15,128,256]{2,3,0,1:T(8,128)(2,1)S(1)}, bf16[2,15,128,256]{2,3,0,1:T(8,128)(2,1)}, u32[]{:S(2)}, u32[]{:S(2)}) collective-permute-start(bf16[2,15,128,256]{2,3,0,1:T(8,128)(2,1)S(1)} %pad_maximum_fusion.2), channel_id=1, source_target_pairs={{0,2},{1,3},{2,0},{3,1},{4,6},{5,7},{6,4},{7,5},{8,10},{9,11},{10,... | collective-permute-start | bytes 5898248 | tf_op jit(solution)/shard_map/ppermute | solution.py:29
  122.8 2.5 copy-start.1
  122.8 10.6 %copy-start.5 = (s32[960]{0:T(1024)S(1)}, s32[960]{0:T(1024)}, u32[]{:S(2)}) copy-start(s32[960]{0:T(1024)} %param.14) | copy-start | bytes 11524
  125.3 177.4 %collective-permute-start.2 = (bf16[4,15,128,256]{2,3,0,1:T(8,128)(2,1)}, bf16[4,15,128,256]{2,3,0,1:T(8,128)(2,1)}, u32[]{:S(2)}, u32[]{:S(2)}) collective-permute-start(bf16[4,15,128,256]{2,3,0,1:T(8,128)(2,1)} %pad_maximum_fusion.1), channel_id=1, source_target_pairs={{0,4},{1,5},{2,6},{3,7},{4,0},{5,1},{6,2},{7,3},{8,12},{9,13},{10,... | collective-permute-start | bytes 11796488 | tf_op jit(solution)/shard_map/ppermute | solution.py:29
  307.8 7.1 %copy-start.4 = (bf16[15,128,256]{2,1,0:T(8,128)(2,1)S(1)}, bf16[15,128,256]{2,1,0:T(8,128)(2,1)}, u32[]{:S(2)}) copy-start(bf16[15,128,256]{2,1,0:T(8,128)(2,1)} %param.8) | copy-start | bytes 2949124
  326.2 12.5 %copy-start.6 = (s32[960]{0:T(1024)S(1)}, s32[960]{0:T(1024)}, u32[]{:S(2)}) copy-start(s32[960]{0:T(1024)} %param.13) | copy-start | bytes 11524
  326.2 110.3 %copy-start.8 = (f32[256,8]{0,1:T(8,128)S(1)}, f32[256,8]{0,1:T(8,128)}, u32[]{:S(2)}) copy-start(f32[256,8]{0,1:T(8,128)} %param.12) | copy-start | bytes 24580
  326.2 110.3 %copy-start.9 = (f32[256]{0:T(256)S(1)}, f32[256]{0:T(256)}, u32[]{:S(2)}) copy-start(f32[256]{0:T(256)} %param.11) | copy-start | bytes 3076
  326.2 107.2 %all-to-all-start = ((bf16[64,128,256]{2,1,0:T(8,128)(2,1)}), bf16[64,128,256]{2,1,0:T(8,128)(2,1)}, u32[]{:S(2)}, u32[]{:S(2)}) async-start(bf16[64,128,256]{2,1,0:T(8,128)(2,1)} %copy.38), calls=%async_computation | async-start | bytes 8388608 | tf_op jit(solution)/shard_map/all_to_all | solution.py:120
  338.6 104.7 %copy-start.7 = (s32[384]{0:T(512)S(1)}, s32[384]{0:T(512)}, u32[]{:S(2)}) copy-start(s32[384]{0:T(512)} %param.15) | copy-start | bytes 4612
  438.1 16.8 %all-to-all-start.1 = ((f32[8,1,11520]{2,1,0:T(1,128)}), f32[8,1,11520]{2,1,0:T(1,128)S(1)}, u32[]{:S(2)}, u32[]{:S(2)}) async-start(f32[8,1,11520]{2,1,0:T(1,128)} %broadcast_in_dim.93), calls=%async_computation.1 | async-start | bytes 737280 | tf_op jit(solution)/shard_map/all_to_all | solution.py:47
  457.0 22.7 %all-to-all-start.2 = ((f32[64,6,8]{2,1,0:T(8,128)}), f32[64,6,8]{2,1,0:T(8,128)S(1)}, u32[]{:S(2)}, u32[]{:S(2)}) async-start(f32[64,6,8]{2,1,0:T(8,128)} %copy.41), calls=%async_computation.2 | async-start | bytes 524288 | tf_op jit(solution)/shard_map/all_to_all | solution.py:70
